TPU v7x, 32 devices: a whole 2x2x4 slice. The times are simulated.
32 devices in a mesh: blk: 8 (over z, x), grp: 4 (over y, core).
Axes of the slice: x: 2, y: 2, z: 4, core: 2. Of those that a mesh axis runs over, the one named last changes fastest.
Arguments:
- positions: float32 [3, 2048], P(None, ('blk', 'grp')), may hold values from -0.25 to 31.25, as said below
- moments: float32 [2, 2, 3, 2048], P(None, None, None, ('blk', 'grp')), may hold values from -6 to 6
- inv_polar_re: float32 [2048], P(('blk', 'grp')), may hold values from 0.5 to 2
- inv_polar_im: float32 [2048], P(('blk', 'grp')), may hold values from -0.5 to 0.5
- mode_field: float32 [2, 3, 2048, 512], P(None, None, ('blk', 'grp')), may hold values from -0.078125 to 0.078125
- mode_detune: float32 [512], replicated, may hold values from -1 to 1
- mode_width: float32 [512], replicated, may hold values from 0.05 to 1
Outputs:
- response: float32 [2, 2, 3, 2048], P(None, None, None, ('blk', 'grp'))
Inputs may be any that keep to these rules, and one draw needn't show every extreme that they name: `positions`: dipole n lies within 0.25, in each coordinate, of the lattice site (n % 32, (n // 32) % 32, n // 1024); distinct dipoles are at least 0.5 apart.
All inputs are finite; a program needn't handle non-finite values.
Results may differ from a plain program's by a relative error of at most 0.0003.
Values sent between devices are 32-bit elements; how exact they have to be, the bound alone decides.
No kernel may reach another device: no remote copies, remote signals or barrier semaphores. Data moves between devices by JAX's collectives and lax.ppermute only.
A program may use at most 64 MiB of HBM per device.

v0:
```python
import math
import jax
import jax.numpy as jnp
from jax import lax
from jax.sharding import PartitionSpec as P

wavenumber = 1.0
coupling = 0.05
near_limit = 0.04


def pair_field(deltas, dipoles, axis_sum):
    delta_x, delta_y, delta_z = deltas
    square = delta_x * delta_x + delta_y * delta_y + delta_z * delta_z
    coincide = square < near_limit
    safe_square = jnp.where(coincide, 1.0, square)
    inverse = 1.0 / jnp.sqrt(safe_square)
    phase_arg = wavenumber * safe_square * inverse
    cos_val = jnp.cos(phase_arg)
    sine_val = jnp.sin(phase_arg)
    masked_cube = jnp.where(coincide, 0.0, inverse * inverse * inverse)
    near_re = phase_arg * phase_arg - 1.0
    far_re = 3.0 - phase_arg * phase_arg
    diag_re = (cos_val * near_re - sine_val * phase_arg) * masked_cube
    diag_im = (sine_val * near_re + cos_val * phase_arg) * masked_cube
    scaled = masked_cube / safe_square
    outer_re = (cos_val * far_re + 3.0 * sine_val * phase_arg) * scaled
    outer_im = (sine_val * far_re - 3.0 * cos_val * phase_arg) * scaled
    tile_list = []
    for drive_set in range(len(dipoles) // 6):
        moment_re = dipoles[6 * drive_set : 6 * drive_set + 3]
        moment_im = dipoles[6 * drive_set + 3 : 6 * drive_set + 6]
        proj_re = delta_x * moment_re[0] + delta_y * moment_re[1] + delta_z * moment_re[2]
        proj_im = delta_x * moment_im[0] + delta_y * moment_im[1] + delta_z * moment_im[2]
        along_re = outer_re * proj_re - outer_im * proj_im
        along_im = outer_re * proj_im + outer_im * proj_re
        for component in range(3):
            tile_list.append(
                diag_re * moment_re[component]
                - diag_im * moment_im[component]
                + deltas[component] * along_re
            )
        for component in range(3):
            tile_list.append(
                diag_re * moment_im[component]
                + diag_im * moment_re[component]
                + deltas[component] * along_im
            )
    return jnp.stack([jnp.sum(entry_tile, axis=axis_sum) for entry_tile in tile_list])


def contract(left, right):
    return lax.dot_general(left, right, (((0,), (1,)), ((), ())), precision=lax.Precision.HIGHEST)


def modal_project(mode_rows, moment_rows):
    amp_re = contract(mode_rows[0], moment_rows[:, 0]) - contract(mode_rows[1], moment_rows[:, 1])
    amp_im = contract(mode_rows[0], moment_rows[:, 1]) + contract(mode_rows[1], moment_rows[:, 0])
    return (amp_re, amp_im)


def spread(weights, rows):
    return lax.dot_general(weights, rows, (((0,), (1,)), ((), ())), precision=lax.Precision.HIGHEST)


def modal_spread(mode_rows, amp_re, amp_im, mode_detune, mode_width):
    denominator = mode_detune * mode_detune + mode_width * mode_width
    resp_re = (mode_detune / denominator)[:, None]
    resp_im = (mode_width / denominator)[:, None]
    weighted_re = resp_re * amp_re - resp_im * amp_im
    weighted_im = resp_re * amp_im + resp_im * amp_re
    out_re = spread(weighted_re, mode_rows[0]) - spread(weighted_im, mode_rows[1])
    out_im = spread(weighted_re, mode_rows[1]) + spread(weighted_im, mode_rows[0])
    return jnp.stack([out_re, out_im], axis=1)


def combine(moments, inv_polar_re, inv_polar_im, pair_part, modal_part):
    drives = moments.shape[0]
    dipole_count = moments.shape[3]
    field_sum = coupling * pair_part.reshape(drives, 2, 3, dipole_count) + modal_part.reshape(
        drives, 2, 3, dipole_count
    )
    moment_re = moments[:, 0]
    moment_im = moments[:, 1]
    resp_re = inv_polar_re * moment_re - inv_polar_im * moment_im - field_sum[:, 0]
    resp_im = inv_polar_re * moment_im + inv_polar_im * moment_re - field_sum[:, 1]
    return jnp.stack([resp_re, resp_im], axis=1)


def on_device(positions, moments, inv_polar_re, inv_polar_im, mode_field, mode_detune, mode_width):
    drives = moments.shape[0]
    dipole_count = positions.shape[1]
    flat_moments = moments.reshape(drives * 6, dipole_count)
    mode_rows = mode_field.reshape(2, 3 * dipole_count, mode_field.shape[3])
    amp_re, amp_im = modal_project(mode_rows, moments.reshape(drives, 2, 3 * dipole_count))
    amp_re, amp_im = lax.psum((amp_re, amp_im), ("blk", "grp"))
    modal_part = modal_spread(mode_rows, amp_re, amp_im, mode_detune, mode_width).reshape(
        drives * 6, dipole_count
    )
    group_pos, group_moments = (
        lax.all_gather(positions, "grp", axis=1, tiled=True),
        lax.all_gather(flat_moments, "grp", axis=1, tiled=True),
    )
    initial = jnp.zeros((drives * 6, dipole_count), jnp.float32)
    places = lax.all_gather(group_pos, "blk", axis=1, tiled=True)
    dipoles = lax.all_gather(group_moments, "blk", axis=1, tiled=True)
    columns = places.shape[1]
    block_width = math.gcd(columns, 2048)

    def advance(block, inner):
        source_pos = lax.dynamic_slice_in_dim(places, block * block_width, block_width, 1)
        source_mom = lax.dynamic_slice_in_dim(dipoles, block * block_width, block_width, 1)
        deltas = [positions[axis_c][:, None] - source_pos[axis_c][None, :] for axis_c in range(3)]
        return inner + pair_field(
            deltas, [source_mom[member][None, :] for member in range(drives * 6)], 1
        )

    pair_part = lax.fori_loop(0, columns // block_width, advance, initial)
    return combine(moments, inv_polar_re, inv_polar_im, pair_part, modal_part)


def solution(mesh):
    placed = (
        P(None, ("blk", "grp")),
        P(None, None, None, ("blk", "grp")),
        P(("blk", "grp")),
        P(("blk", "grp")),
        P(None, None, ("blk", "grp"), None),
        P(),
        P(),
    )
    return jax.shard_map(
        on_device,
        mesh=mesh,
        in_specs=placed,
        out_specs=P(None, None, None, ("blk", "grp")),
        check_vma=False,
    )
```

profile of v0, /device:TPU:0, one launch (start us, length us, event | category | flops | bytes accessed | tf_op | source)
XLA Modules:
  0.0 126.5 jit_solution(16070612129556951673)
XLA Ops:
  0.0 0.0 copy-start.1
  0.0 1.2 fusion.63
  1.2 0.0 copy-done.1
  1.2 0.1 reshape.26
  1.3 0.3 fusion.53
  1.6 0.3 convolution_subtract_fusion
  1.9 0.3 fusion.49
  2.3 0.3 convolution_add_fusion
  2.6 42.1 %all-reduce = (f32[512,2]{0,1:T(2,128)S(1)}, f32[512,2]{0,1:T(2,128)S(1)}) all-reduce(f32[512,2]{0,1:T(2,128)S(1)} %convolution_add_fusion, f32[512,2]{0,1:T(2,128)S(1)} %convolution_subtract_fusion), channel_id=1, replica_groups=mesh['blk'=8,'grp'=4] {'blk','grp'}, use_global_device_ids=true, to_apply=%region_13.0 | all-reduce | flops 2048 | bytes 16384 | tf_op jit(solution)/shard_map/psum | solution.py:96
  44.7 0.0 copy-done.3
  44.7 0.7 copy-done.2
  45.4 0.4 fusion.62
  45.8 0.4 convolution_subtract_fusion.1
  46.2 0.1 stack.79
  46.3 0.4 fusion.61
  46.7 0.4 convolution_add_fusion.1
  47.1 0.1 stack.80
  47.2 5.5 %all-gather.1 = f32[4,64,12]{1,2,0:T(8,128)S(1)} all-gather(f32[1,64,12]{1,2,0:T(8,128)S(1)} %bitcast.76), channel_id=1, replica_groups=mesh['blk'=8,'grp'=4] {'grp'}, dimensions={0}, use_global_device_ids=true | all-gather | bytes 15360 | tf_op jit(solution)/shard_map/all_gather | solution.py:102
  52.8 0.1 reshape.30
  52.9 30.5 %all_gather.15 = f32[12,2048]{1,0:T(8,128)S(1)} all-gather(f32[12,256]{1,0:T(8,128)S(1)} %bitcast.75), channel_id=1, replica_groups=mesh['blk'=8,'grp'=4] {'blk'}, dimensions={1}, use_global_device_ids=true | all-gather | bytes 110592 | tf_op jit(solution)/shard_map/all_gather | solution.py:106
  83.4 0.1 fusion.64
  83.4 0.0 copy-start
  83.5 0.7 copy-done
  84.1 5.2 %all-gather = f32[4,64,3]{1,2,0:T(4,128)S(1)} all-gather(f32[1,64,3]{1,2,0:T(4,128)S(1)} %bitcast.95), channel_id=1, replica_groups=mesh['blk'=8,'grp'=4] {'grp'}, dimensions={0}, use_global_device_ids=true | all-gather | bytes 3840 | tf_op jit(solution)/shard_map/all_gather | solution.py:101
  89.3 0.1 reshape.28
  89.4 30.6 %all_gather.13 = f32[3,2048]{1,0:T(4,128)S(1)} all-gather(f32[3,256]{1,0:T(4,128)S(1)} %bitcast.77), channel_id=1, replica_groups=mesh['blk'=8,'grp'=4] {'blk'}, dimensions={1}, use_global_device_ids=true | all-gather | bytes 27648 | tf_op jit(solution)/shard_map/all_gather | solution.py:105
  120.0 5.1 %fusion.45 = (f32[64]{0:T(128)S(1)}, f32[64]{0:T(128)S(1)}, f32[64]{0:T(128)S(1)}, f32[64]{0:T(128)S(1)}, f32[64]{0:T(128)S(1)}, /*index=5*/f32[64]{0:T(128)S(1)...) fusion(f32[2048]{0:T(1024)S(1)} %bitcast.81, ...), kind=kLoop, calls=%fused_computation.80 | loop fusion | flops 18349312 | bytes 126720 | tf_op jit(solution)/shard_map/while/body/eval_jaxpr/reduce_sum | solution.py:49
  125.2 0.0 copy-start.4
  125.2 0.0 copy-start.5
  125.2 0.6 copy-done.4
  125.9 0.0 copy-done.5
  125.9 0.6 copy.37
  (16 shorter events, 0.2 us)
Async XLA Ops:
  0.0 1.2 copy-start.1
  2.6 42.1 %copy-start.3 = (f32[512]{0:T(512)S(1)}, f32[512]{0:T(512)}, u32[]{:S(2)}) copy-start(f32[512]{0:T(512)} %param.13) | copy-start | bytes 6148
  44.7 0.7 copy-start.2
  83.4 0.7 copy-start
  125.2 0.7 copy-start.4
  125.2 0.7 copy-start.5
where the time goes:
time: 127 us; the launch traced here: 126 us
  blocking collectives  114 us (90%)
  other arithmetic  5.14 us (4%)
  local copies, waits for them, and re-layouts  4.42 us (3%)
  matrix products  2.95 us (2%)
    psum x1, blocking collectives, on_device(): amp_re, amp_im = lax.psum((amp_re, amp_im), ('blk', 'grp'))  42.1 us
    all_gather x1, blocking collectives, on_device(): places = lax.all_gather(group_pos, 'blk', axis=1, tiled=True)  30.6 us
    all_gather x1, blocking collectives, on_device(): dipoles = lax.all_gather(group_moments, 'blk', axis=1, tiled=True)  30.5 us
    all_gather x1, blocking collectives, on_device(): lax.all_gather(flat_moments, 'grp', axis=1, tiled=True)  5.52 us
    all_gather x1, blocking collectives, on_device(): lax.all_gather(positions, 'grp', axis=1, tiled=True)  5.18 us
    reduce_sum x1, other arithmetic, pair_field(): jnp.sum(entry_tile, axis=axis_sum)  5.11 us

commit v1 on v0

--- a/solution.py
+++ b/solution.py
@@ -102,8 +102,13 @@
         lax.all_gather(flat_moments, "grp", axis=1, tiled=True),
     )
     initial = jnp.zeros((drives * 6, dipole_count), jnp.float32)
-    places = lax.all_gather(group_pos, "blk", axis=1, tiled=True)
-    dipoles = lax.all_gather(group_moments, "blk", axis=1, tiled=True)
+    places, dipoles = jnp.split(
+        lax.all_gather(
+            jnp.concatenate([group_pos, group_moments], axis=0), axis=1, tiled=True, axis_name="blk"
+        ),
+        [group_pos.shape[0]],
+        axis=0,
+    )
     columns = places.shape[1]
     block_width = math.gcd(columns, 2048)
 

time: 127 us -> 96.5 us (0.76)
  blocking collectives: 114 us -> 83.5 us
    all_gather x2 -> x1, blocking collectives: 61.1 us -> 30.5 us  [on_device(): lax.all_gather(jnp.concatenate([group_pos, group_moments], axis=0), axis=...]
where the time goes in v1:
time: 96.5 us; the launch traced here: 96.1 us
  blocking collectives  83.5 us (87%)
  other arithmetic  5.15 us (5%)
  local copies, waits for them, and re-layouts  4.42 us (5%)
  matrix products  2.95 us (3%)
    psum x1, blocking collectives, on_device(): amp_re, amp_im = lax.psum((amp_re, amp_im), ('blk', 'grp'))  42.1 us
    all_gather x1, blocking collectives, on_device(): lax.all_gather(jnp.concatenate([group_pos, group_moments], axis=0), axis=...  30.5 us
    all_gather x1, blocking collectives, on_device(): lax.all_gather(flat_moments, 'grp', axis=1, tiled=True)  5.52 us
    all_gather x1, blocking collectives, on_device(): lax.all_gather(positions, 'grp', axis=1, tiled=True)  5.42 us
    reduce_sum x1, other arithmetic, pair_field(): jnp.sum(entry_tile, axis=axis_sum)  5.11 us
    unnamed x15, local copies, waits for them, and re-layouts  2.18 us

profile of v1, /device:TPU:0, one launch (start us, length us, event | category | flops | bytes accessed | tf_op | source)
XLA Modules:
  0.0 96.1 jit_solution(16674815038808664368)
XLA Ops:
  0.0 0.0 copy-start.1
  0.0 1.2 %fusion.63 = (f32[1,3,64,512]{3,2,1,0:T(8,128)S(1)}, f32[1,3,64,512]{3,2,1,0:T(8,128)S(1)}) fusion(f32[2,3,64,512]{3,2,1,0:T(8,128)} %param.11), kind=kLoop, calls=%fused_computation.115 | loop fusion | bytes 1572864 | tf_op jit(solution)/shard_map/slice | solution.py:57
  1.2 0.0 copy-done.1
  1.2 0.1 reshape.26
  1.3 0.3 fusion.53
  1.6 0.3 convolution_subtract_fusion
  1.9 0.3 fusion.49
  2.3 0.3 convolution_add_fusion
  2.6 0.0 copy-start.3
  2.6 42.1 %all-reduce = (f32[512,2]{0,1:T(2,128)S(1)}, f32[512,2]{0,1:T(2,128)S(1)}) all-reduce(f32[512,2]{0,1:T(2,128)S(1)} %convolution_add_fusion, f32[512,2]{0,1:T(2,128)S(1)} %convolution_subtract_fusion), channel_id=1, replica_groups=mesh['blk'=8,'grp'=4] {'blk','grp'}, use_global_device_ids=true, to_apply=%region_13.0 | all-reduce | flops 2048 | bytes 16384 | tf_op jit(solution)/shard_map/psum | solution.py:96
  44.7 0.0 copy-start.2
  44.7 0.0 copy-done.3
  44.7 0.7 copy-done.2
  45.4 0.4 fusion.62
  45.8 0.4 convolution_subtract_fusion.1
  46.2 0.1 stack.79
  46.3 0.4 fusion.61
  46.7 0.4 convolution_add_fusion.1
  47.1 0.1 stack.80
  47.2 5.5 %all-gather.1 = f32[4,64,12]{1,2,0:T(8,128)S(1)} all-gather(f32[1,64,12]{1,2,0:T(8,128)S(1)} %bitcast.76), channel_id=1, replica_groups=mesh['blk'=8,'grp'=4] {'grp'}, dimensions={0}, use_global_device_ids=true | all-gather | bytes 15360 | tf_op jit(solution)/shard_map/all_gather | solution.py:102
  52.8 0.1 reshape.30
  52.9 0.7 copy-done
  53.5 5.4 %all-gather = f32[4,64,3]{1,2,0:T(4,128)S(1)} all-gather(f32[1,64,3]{1,2,0:T(4,128)S(1)} %bitcast.95), channel_id=1, replica_groups=mesh['blk'=8,'grp'=4] {'grp'}, dimensions={0}, use_global_device_ids=true | all-gather | bytes 3840 | tf_op jit(solution)/shard_map/all_gather | solution.py:101
  59.0 0.1 reshape.28
  59.1 30.5 %all_gather.11 = f32[15,2048]{1,0:T(8,128)S(1)} all-gather(f32[15,256]{1,0:T(8,128)S(1)} %pad_maximum_fusion), channel_id=1, replica_groups=mesh['blk'=8,'grp'=4] {'blk'}, dimensions={1}, use_global_device_ids=true | all-gather | bytes 138240 | tf_op jit(solution)/shard_map/all_gather | solution.py:106
  89.6 0.1 fusion.64
  89.7 5.1 %fusion.45 = (f32[64]{0:T(128)S(1)}, f32[64]{0:T(128)S(1)}, f32[64]{0:T(128)S(1)}, f32[64]{0:T(128)S(1)}, f32[64]{0:T(128)S(1)}, /*index=5*/f32[64]{0:T(128)S(1)...) fusion(f32[2048]{0:T(1024)S(1)} %bitcast.81, ...), kind=kLoop, calls=%fused_computation.80 | loop fusion | flops 18349312 | bytes 126720 | tf_op jit(solution)/shard_map/while/body/eval_jaxpr/reduce_sum | solution.py:49
  94.9 0.0 copy-start.4
  94.9 0.0 copy-start.5
  94.9 0.6 copy-done.4
  95.5 0.0 copy-done.5
  95.5 0.6 copy.37
  (15 shorter events, 0.1 us)
Async XLA Ops:
  0.0 1.2 %copy-start.1 = (f32[2,2,3,64]{3,1,2,0:T(2,128)S(1)}, f32[2,2,3,64]{3,1,2,0:T(2,128)}, u32[]{:S(2)}) copy-start(f32[2,2,3,64]{3,1,2,0:T(2,128)} %param.8) | copy-start | bytes 9220
  2.6 42.1 %copy-start.3 = (f32[512]{0:T(512)S(1)}, f32[512]{0:T(512)}, u32[]{:S(2)}) copy-start(f32[512]{0:T(512)} %param.13) | copy-start | bytes 6148
  44.7 0.7 copy-start.2
  52.9 0.7 copy-start
  94.9 0.7 copy-start.4
  94.9 0.7 copy-start.5
